TPU v7x, 256 devices: a whole 4x4x8 slice. The times are simulated.
256 devices in a mesh: dp: 8 (over x, y_lo), tp: 32 (over y_hi, z, core).
Axes of the slice: x: 4, y: 4 (y_hi: 2, y_lo: 2; y = y_hi * 2 + y_lo), z: 8, core: 2. Of those that a mesh axis runs over, the one named last changes fastest.
Arguments:
- proj_in: bfloat16 [1, 32768, 8192], P(None, 'dp', 'tp'), may hold values from -6 to 6
- kv_grad: bfloat16 [1, 32768, 2048], P(None, ('dp', 'tp')), may hold values from -0.75 to 0.75
- normed: bfloat16 [1, 32768, 8192], P(None, ('dp', 'tp')), may hold values from -6 to 6
- norm_grad: bfloat16 [1, 32768, 8192], P(None, ('dp', 'tp')), may hold values from -0.6 to 0.6
- first_moment: float32 [1, 8192, 2048], P(None, 'tp', 'dp'), may hold values from -0.6 to 0.6
- second_moment: float32 [1, 8192, 2048], P(None, 'tp', 'dp'), may hold values from 0.002 to 0.02
Outputs:
- new_first: float32 [1, 8192, 2048], P(None, 'tp', 'dp')
- new_second: float32 [1, 8192, 2048], P(None, 'tp', 'dp')
- adam_step: float32 [1, 8192, 2048], P(None, 'tp', 'dp')
- gain_grad: float32 [1, 8192], replicated
All inputs are finite; a program needn't handle non-finite values.
Results may differ from a plain program's by a relative error of at most 0.0003.
Values may be sent and summed in bfloat16 or wider, within the bound.
A program may use at most 128 MiB of HBM per device.

v0:
```python
import functools
import jax
import jax.numpy as jnp
from jax import lax
from jax.sharding import Mesh
from jax.sharding import PartitionSpec as P

DP = ("dp_0", "dp_1")
DP_TP = ("dp_0", "dp_1", "tp_0", "tp_1", "tp_2")
TP = ("tp_0", "tp_1", "tp_2")
beta_one = 0.9
beta_two = 0.95
correct_one = 0.19
correct_two = 0.0975
epsilon = 1e-08


def over_axes(array, axes):
    return functools.reduce(lax.psum, axes, array)


def in_blocks(array, dim, size):
    lengths = array.shape
    pieces = array.reshape(*lengths[:dim], size, lengths[dim] // size, *lengths[dim + 1 :])
    return jnp.moveaxis(pieces, dim, 0)


def sent_and_summed(array, axis, dim):
    pieces = in_blocks(array, dim, lax.axis_size(axis))
    arrived = lax.all_to_all(pieces, axis, split_axis=0, concat_axis=0, tiled=True)
    return arrived.sum(axis=0)


def adam_update(mean_grad, first_old, second_old):
    new_first = beta_one * first_old + (1.0 - beta_one) * mean_grad
    new_second = beta_two * second_old + (1.0 - beta_two) * mean_grad * mean_grad
    update = new_first / correct_one / (jnp.sqrt(new_second / correct_two) + epsilon)
    return (new_first, new_second, update)


def row_adder(inputs, arrived):
    return lax.dot_general(
        inputs, arrived, (((0,), (0,)), ((), ())), preferred_element_type=jnp.float32
    )


def shards(proj_in, kv_grad, normed, norm_grad, first_moment, second_moment):
    replicas = lax.axis_size(DP)
    local_terms = jnp.sum(norm_grad.astype(jnp.float32) * normed.astype(jnp.float32), axis=1)
    gain_grad = over_axes(local_terms, DP_TP) / replicas
    inputs = proj_in[0]
    grad_rows = kv_grad[0]
    local_grad = row_adder(inputs, lax.all_gather(grad_rows, TP, axis=0, tiled=True))
    mean_grad = sent_and_summed(local_grad, DP, 1) / replicas
    new_first, new_second, update = adam_update(mean_grad, first_moment[0], second_moment[0])
    firsts = [new_first]
    seconds = [new_second]
    updates = [update]
    return (jnp.stack(firsts), jnp.stack(seconds), jnp.stack(updates), gain_grad)


def solution(mesh):
    finer = Mesh(mesh.devices.reshape(4, 2, 2, 8, 2), ("dp_0", "dp_1", "tp_0", "tp_1", "tp_2"))
    return jax.shard_map(
        shards,
        mesh=finer,
        in_specs=(
            P(None, DP, TP),
            P(None, DP_TP, None),
            P(None, DP_TP, None),
            P(None, DP_TP, None),
            P(None, TP, DP),
            P(None, TP, DP),
        ),
        out_specs=(P(None, TP, DP), P(None, TP, DP), P(None, TP, DP), P()),
        check_vma=False,
    )
```

profile of v0, /device:TPU:1, one launch (start us, length us, event | category | flops | bytes accessed | tf_op | source)
XLA Modules:
  0.0 229.3 jit_solution(13198261550055182338)
XLA Ops:
  7.2 0.0 copy-start
  7.2 0.0 all-gather.3.cloned.1.call-start
  7.2 0.7 all-gather.3.cloned.1.call-update
  7.9 2.8 %multiply_reduce_fusion = f32[8192]{0:T(1024)S(1)} fusion(bf16[1,128,8192]{2,1,0:T(8,128)(2,1)} %param.8, bf16[1,128,8192]{2,1,0:T(8,128)(2,1)} %param.9), kind=kLoop, calls=%fused_computation | loop fusion | flops 4186112 | bytes 4227072 | tf_op jit(solution)/shard_map/reduce_sum | solution.py:49
  10.7 14.3 %psum.35 = f32[1,8192]{1,0:T(1,128)S(1)} all-reduce(f32[1,8192]{1,0:T(1,128)S(1)} %bitcast.23), channel_id=1, replica_groups=mesh['dp_0'=4,'dp_1'=2,'tp_0'=2,'tp_1'=8,'tp_2'=2] {'dp_0'}, use_global_device_ids=true, to_apply=%region_2.0 | all-reduce | flops 8192 | bytes 65536 | tf_op jit(solution)/shard_map/psum | solution.py:19
  25.1 7.0 %psum.36 = f32[1,8192]{1,0:T(1,128)S(1)} all-reduce(f32[1,8192]{1,0:T(1,128)S(1)} %psum.35), channel_id=1, replica_groups=mesh['dp_0'=4,'dp_1'=2,'tp_0'=2,'tp_1'=8,'tp_2'=2] {'dp_1'}, use_global_device_ids=true, to_apply=%region_3.0 | all-reduce | flops 8192 | bytes 65536 | tf_op jit(solution)/shard_map/psum | solution.py:19
  32.1 9.2 %psum.37 = f32[1,8192]{1,0:T(1,128)S(1)} all-reduce(f32[1,8192]{1,0:T(1,128)S(1)} %psum.36), channel_id=1, replica_groups=mesh['dp_0'=4,'dp_1'=2,'tp_0'=2,'tp_1'=8,'tp_2'=2] {'tp_0'}, use_global_device_ids=true, to_apply=%region_4.0 | all-reduce | flops 8192 | bytes 65536 | tf_op jit(solution)/shard_map/psum | solution.py:19
  41.3 111.2 %all-gather.3.cloned.1.call-done = bf16[1,4096,2048]{2,1,0:T(8,128)(2,1)} async-done(((bf16[1,128,2048]{2,1,0:T(8,128)(2,1)}), bf16[1,4096,2048]{2,1,0:T(8,128)(2,1)}) %all-gather.3.cloned.1.call-update) | async-done | bytes 16777232 | tf_op jit(solution)/shard_map/all_gather | solution.py:53
  152.5 20.7 %copy.10 = bf16[2048,4096]{1,0:T(8,128)(2,1)} copy(bf16[2048,4096]{0,1:T(8,128)(2,1)} %bitcast.21) | data formatting | bytes 33554432 | tf_op jit(solution)/shard_map/dot_general | solution.py:42
  173.3 0.0 copy-done
  173.3 9.5 %fusion.2 = f32[8,256,256]{2,1,0:T(8,128)} fusion(bf16[8,256,4096]{2,1,0:T(8,128)(2,1)} %bitcast.22, bf16[1,4096,256]{2,1,0:T(8,128)(2,1)S(1)} %copy-done), kind=kOutput, calls=%fused_computation.3 | convolution fusion | flops 4294967296 | bytes 20971520 | tf_op jit(solution)/shard_map/dot_general | solution.py:42
  182.8 4.3 %all-to-all-start = ((f32[8,256,256]{2,1,0:T(8,128)}), f32[8,256,256]{2,1,0:T(8,128)}, u32[]{:S(2)}, u32[]{:S(2)}) async-start(f32[8,256,256]{2,1,0:T(8,128)} %fusion.2), calls=%async_computation | async-start | bytes 4194304 | tf_op jit(solution)/shard_map/all_to_all | solution.py:30
  187.1 0.0 copy-start.1
  187.2 0.0 copy-start.2
  187.2 24.0 %psum.38 = f32[1,8192]{1,0:T(1,128)S(1)} all-reduce(f32[1,8192]{1,0:T(1,128)S(1)} %psum.37), channel_id=1, replica_groups=mesh['dp_0'=4,'dp_1'=2,'tp_0'=2,'tp_1'=8,'tp_2'=2] {'tp_1'}, use_global_device_ids=true, to_apply=%region_5.0 | all-reduce | flops 8192 | bytes 65536 | tf_op jit(solution)/shard_map/psum | solution.py:19
  211.1 7.9 %psum.39 = f32[1,8192]{1,0:T(1,128)S(1)} all-reduce(f32[1,8192]{1,0:T(1,128)S(1)} %psum.38), channel_id=1, replica_groups=mesh['dp_0'=4,'dp_1'=2,'tp_0'=2,'tp_1'=8,'tp_2'=2] {'tp_2'}, use_global_device_ids=true, to_apply=%region_6.0 | all-reduce | flops 8192 | bytes 65536 | tf_op jit(solution)/shard_map/psum | solution.py:19
  219.1 0.6 broadcast_multiply_fusion
  219.7 0.0 all-to-all-done
  219.7 1.8 reduce_sum.20
  221.5 0.0 copy-done.1
  221.5 0.0 copy-done.2
  221.5 1.0 add_divide_fusion
Async XLA Ops:
  7.2 166.1 %copy-start = (bf16[1,4096,256]{2,1,0:T(8,128)(2,1)S(1)}, bf16[1,4096,256]{2,1,0:T(8,128)(2,1)}, u32[]{:S(2)}) copy-start(bf16[1,4096,256]{2,1,0:T(8,128)(2,1)} %param.6) | copy-start | bytes 6291460
  7.2 145.3 %all-gather.3.cloned.1.call-start = ((), (), s32[]{:S(2)}) async-start(), calls=%async_computation.1 | async-start | bytes 17301504 | tf_op jit(solution)/shard_map/all_gather | solution.py:53
  182.8 36.9 %all-to-all-start = ((f32[8,256,256]{2,1,0:T(8,128)}), f32[8,256,256]{2,1,0:T(8,128)}, u32[]{:S(2)}, u32[]{:S(2)}) async-start(f32[8,256,256]{2,1,0:T(8,128)} %fusion.2), calls=%async_computation | async-start | bytes 4194304 | tf_op jit(solution)/shard_map/all_to_all | solution.py:30
  187.1 34.3 %copy-start.1 = (f32[1,256,256]{2,1,0:T(8,128)S(1)}, f32[1,256,256]{2,1,0:T(8,128)}, u32[]{:S(2)}) copy-start(f32[1,256,256]{2,1,0:T(8,128)} %param.11) | copy-start | bytes 786436
  187.2 34.3 %copy-start.2 = (f32[1,256,256]{2,1,0:T(8,128)S(1)}, f32[1,256,256]{2,1,0:T(8,128)}, u32[]{:S(2)}) copy-start(f32[1,256,256]{2,1,0:T(8,128)} %param.10) | copy-start | bytes 786436
Sparse Core Ops, SparseCore 0:
  10.8 141.7 all-gather.2
where the time goes:
time: 230 us; the launch traced here: 229 us
  waiting for transfers between devices  112 us (49%)
  blocking collectives  62.4 us (27%)
  local copies, waits for them, and re-layouts  20.8 us (9%)
  between operations  14.1 us (6%)
  matrix products  9.54 us (4%)
  other arithmetic  6.19 us (3%)
  starting transfers between devices  4.38 us (2%)
    all_gather x1, waiting for transfers between devices, shards(): lax.all_gather(grad_rows, TP, axis=0, tiled=True)  111 us
    psum x5, blocking collectives, over_axes(): return functools.reduce(lax.psum, axes, array)  62.4 us
    dot_general x1, local copies, waits for them, and re-layouts, row_adder(): lax.dot_general(inputs, arrived, (((0,), (0,)), ((), ())), preferred_elem...  20.7 us
    dot_general x1, matrix products, row_adder(): lax.dot_general(inputs, arrived, (((0,), (0,)), ((), ())), preferred_elem...  9.54 us
  transfers between devices with their start and end apart: 2, of which 1 were waited for; matrix products, arithmetic and copies ran while one was open for 2% of the time, Pallas kernels for 0%

commit v1 on v0

--- a/solution.py
+++ b/solution.py
@@ -13,6 +13,13 @@
 correct_one = 0.19
 correct_two = 0.0975
 epsilon = 1e-08
+
+
+def all_by_exchange(x, name, dim):
+    devices = lax.axis_size(name)
+    parts = jnp.stack([x for _ in range(devices)])
+    parts = lax.all_to_all(parts, name, split_axis=0, concat_axis=0)
+    return jnp.concatenate(parts, axis=dim)
 
 
 def over_axes(array, axes):
@@ -50,7 +57,7 @@
     gain_grad = over_axes(local_terms, DP_TP) / replicas
     inputs = proj_in[0]
     grad_rows = kv_grad[0]
-    local_grad = row_adder(inputs, lax.all_gather(grad_rows, TP, axis=0, tiled=True))
+    local_grad = row_adder(inputs, all_by_exchange(grad_rows, TP, 0))
     mean_grad = sent_and_summed(local_grad, DP, 1) / replicas
     new_first, new_second, update = adam_update(mean_grad, first_moment[0], second_moment[0])
     firsts = [new_first]

time: 230 us -> 488 us (2.12)
  waiting for transfers between devices: 112 us -> 316 us
  local copies, waits for them, and re-layouts: 20.8 us -> 51 us
  blocking collectives: 62.4 us -> 86.5 us
  between operations: 14.1 us -> 0.73 us
  starting transfers between devices: 4.38 us -> 17.1 us
    all_to_all x0 -> x1, waiting for transfers between devices: none -> 316 us  [all_by_exchange(): parts = lax.all_to_all(parts, name, split_axis=0, concat_axis=0)]
    all_gather x1 -> x0, waiting for transfers between devices: 111 us -> none  [shards(): lax.all_gather(grad_rows, TP, axis=0, tiled=True)]
    psum x5, blocking collectives: 62.4 us -> 86.5 us  [over_axes(): return functools.reduce(lax.psum, axes, array)]
    all_to_all x0 -> x1, local copies, waits for them, and re-layouts: none -> 22.6 us  [all_by_exchange(): parts = lax.all_to_all(parts, name, split_axis=0, concat_axis=0)]
    all_to_all x0 -> x1, starting transfers between devices: none -> 12.8 us  [all_by_exchange(): parts = lax.all_to_all(parts, name, split_axis=0, concat_axis=0)]
    another operation x0 -> x2, local copies, waits for them, and re-layouts: none -> 7.66 us  [the longest x1 6.21 us: all_by_exchange(): parts = jnp.stack([x for _ in range(devices)])]
  transfers between devices with their start and end apart: 2 -> 2, of which waited for: 1 -> 1; matrix products, arithmetic and copies ran while one was open for 2% -> 1% of each run, Pallas kernels for 0% -> 0%
where the time goes in v1:
time: 488 us; the launch traced here: 487 us
  waiting for transfers between devices  316 us (65%)
  blocking collectives  86.5 us (18%)
  local copies, waits for them, and re-layouts  51 us (10%)
  starting transfers between devices  17.1 us (4%)
  matrix products  9.54 us (2%)
  other arithmetic  6.19 us (1%)
    all_to_all x1, waiting for transfers between devices, all_by_exchange(): parts = lax.all_to_all(parts, name, split_axis=0, concat_axis=0)  316 us
    psum x5, blocking collectives, over_axes(): return functools.reduce(lax.psum, axes, array)  86.5 us
    all_to_all x1, local copies, waits for them, and re-layouts, all_by_exchange(): parts = lax.all_to_all(parts, name, split_axis=0, concat_axis=0)  22.6 us
    dot_general x1, local copies, waits for them, and re-layouts, row_adder(): lax.dot_general(inputs, arrived, (((0,), (0,)), ((), ())), preferred_elem...  20.7 us
    all_to_all x1, starting transfers between devices, all_by_exchange(): parts = lax.all_to_all(parts, name, split_axis=0, concat_axis=0)  12.8 us
  transfers between devices with their start and end apart: 2, of which 1 were waited for; matrix products, arithmetic and copies ran while one was open for 1% of the time, Pallas kernels for 0%

profile of v1, /device:TPU:1, one launch (start us, length us, event | category | flops | bytes accessed | tf_op | source)
XLA Modules:
  0.0 486.7 jit_solution(9427068252237209626)
XLA Ops:
  0.6 0.0 copy-start
  0.6 1.5 copy.14
  2.1 6.2 %stack.2 = bf16[32,128,2048]{1,2,0:T(8,128)(2,1)} broadcast(bf16[128,2048]{0,1:T(8,128)(2,1)S(1)} %copy.14), dimensions={1,2} | broadcast | bytes 17301504 | tf_op jit(solution)/shard_map/stack | solution.py:20
  8.3 12.8 %all-to-all-start = ((bf16[32,128,2048]{1,2,0:T(8,128)(2,1)}), bf16[32,128,2048]{1,2,0:T(8,128)(2,1)}, u32[]{:S(2)}, u32[]{:S(2)}) async-start(bf16[32,128,2048]{1,2,0:T(8,128)(2,1)} %stack.2), calls=%async_computation | async-start | bytes 33554432 | tf_op jit(solution)/shard_map/all_to_all | solution.py:21
  21.1 2.8 multiply_reduce_fusion
  24.0 14.9 %psum.35 = f32[1,8192]{1,0:T(1,128)S(1)} all-reduce(f32[1,8192]{1,0:T(1,128)S(1)} %bitcast.25), channel_id=1, replica_groups=mesh['dp_0'=4,'dp_1'=2,'tp_0'=2,'tp_1'=8,'tp_2'=2] {'dp_0'}, use_global_device_ids=true, to_apply=%region_2.0 | all-reduce | flops 8192 | bytes 65536 | tf_op jit(solution)/shard_map/psum | solution.py:26
  38.9 14.5 %psum.36 = f32[1,8192]{1,0:T(1,128)S(1)} all-reduce(f32[1,8192]{1,0:T(1,128)S(1)} %psum.35), channel_id=1, replica_groups=mesh['dp_0'=4,'dp_1'=2,'tp_0'=2,'tp_1'=8,'tp_2'=2] {'dp_1'}, use_global_device_ids=true, to_apply=%region_3.0 | all-reduce | flops 8192 | bytes 65536 | tf_op jit(solution)/shard_map/psum | solution.py:26
  53.4 14.9 %psum.37 = f32[1,8192]{1,0:T(1,128)S(1)} all-reduce(f32[1,8192]{1,0:T(1,128)S(1)} %psum.36), channel_id=1, replica_groups=mesh['dp_0'=4,'dp_1'=2,'tp_0'=2,'tp_1'=8,'tp_2'=2] {'tp_0'}, use_global_device_ids=true, to_apply=%region_4.0 | all-reduce | flops 8192 | bytes 65536 | tf_op jit(solution)/shard_map/psum | solution.py:26
  68.3 315.6 %all-to-all-done = bf16[32,128,2048]{1,2,0:T(8,128)(2,1)} async-done(((bf16[32,128,2048]{1,2,0:T(8,128)(2,1)}), bf16[32,128,2048]{1,2,0:T(8,128)(2,1)}, u32[]{:S(2)}, u32[]{:S(2)}) %all-to-all-start) | async-done | bytes 16777248 | tf_op jit(solution)/shard_map/all_to_all | solution.py:21
  383.8 22.6 %copy.15 = bf16[32,128,2048]{2,1,0:T(8,128)(2,1)} copy(bf16[32,128,2048]{1,2,0:T(8,128)(2,1)} %all-to-all-done) | data formatting | bytes 33554432 | tf_op jit(solution)/shard_map/all_to_all | solution.py:21
  406.4 20.7 %copy.16 = bf16[2048,4096]{1,0:T(8,128)(2,1)} copy(bf16[2048,4096]{0,1:T(8,128)(2,1)} %bitcast.22) | data formatting | bytes 33554432 | tf_op jit(solution)/shard_map/dot_general | solution.py:49
  427.2 0.0 copy-done
  427.2 9.5 %fusion.2 = f32[8,256,256]{2,1,0:T(8,128)} fusion(bf16[8,256,4096]{2,1,0:T(8,128)(2,1)} %bitcast.23, bf16[1,4096,256]{2,1,0:T(8,128)(2,1)S(1)} %copy-done), kind=kOutput, calls=%fused_computation.3 | convolution fusion | flops 4294967296 | bytes 20971520 | tf_op jit(solution)/shard_map/dot_general | solution.py:49
  436.7 4.3 all-to-all-start.1
  441.1 0.0 copy-start.1
  441.1 0.0 copy-start.2
  441.1 33.3 %psum.38 = f32[1,8192]{1,0:T(1,128)S(1)} all-reduce(f32[1,8192]{1,0:T(1,128)S(1)} %psum.37), channel_id=1, replica_groups=mesh['dp_0'=4,'dp_1'=2,'tp_0'=2,'tp_1'=8,'tp_2'=2] {'tp_1'}, use_global_device_ids=true, to_apply=%region_5.0 | all-reduce | flops 8192 | bytes 65536 | tf_op jit(solution)/shard_map/psum | solution.py:26
  474.4 8.8 %psum.39 = f32[1,8192]{1,0:T(1,128)S(1)} all-reduce(f32[1,8192]{1,0:T(1,128)S(1)} %psum.38), channel_id=1, replica_groups=mesh['dp_0'=4,'dp_1'=2,'tp_0'=2,'tp_1'=8,'tp_2'=2] {'tp_2'}, use_global_device_ids=true, to_apply=%region_6.0 | all-reduce | flops 8192 | bytes 65536 | tf_op jit(solution)/shard_map/psum | solution.py:26
  483.3 0.6 broadcast_multiply_fusion
  483.9 0.0 all-to-all-done.1
  483.9 1.8 reduce_sum.20
  485.7 0.0 copy-done.1
  485.7 0.0 copy-done.2
  485.7 1.0 add_divide_fusion
Async XLA Ops:
  0.6 426.5 %copy-start = (bf16[1,4096,256]{2,1,0:T(8,128)(2,1)S(1)}, bf16[1,4096,256]{2,1,0:T(8,128)(2,1)}, u32[]{:S(2)}) copy-start(bf16[1,4096,256]{2,1,0:T(8,128)(2,1)} %param.6) | copy-start | bytes 6291460
  8.3 375.5 %all-to-all-start = ((bf16[32,128,2048]{1,2,0:T(8,128)(2,1)}), bf16[32,128,2048]{1,2,0:T(8,128)(2,1)}, u32[]{:S(2)}, u32[]{:S(2)}) async-start(bf16[32,128,2048]{1,2,0:T(8,128)(2,1)} %stack.2), calls=%async_computation | async-start | bytes 33554432 | tf_op jit(solution)/shard_map/all_to_all | solution.py:21
  436.7 47.2 %all-to-all-start.1 = ((f32[8,256,256]{2,1,0:T(8,128)}), f32[8,256,256]{2,1,0:T(8,128)}, u32[]{:S(2)}, u32[]{:S(2)}) async-start(f32[8,256,256]{2,1,0:T(8,128)} %fusion.2), calls=%async_computation.1 | async-start | bytes 4194304 | tf_op jit(solution)/shard_map/all_to_all | solution.py:37
  441.1 44.6 %copy-start.1 = (f32[1,256,256]{2,1,0:T(8,128)S(1)}, f32[1,256,256]{2,1,0:T(8,128)}, u32[]{:S(2)}) copy-start(f32[1,256,256]{2,1,0:T(8,128)} %param.11) | copy-start | bytes 786436
  441.1 44.6 %copy-start.2 = (f32[1,256,256]{2,1,0:T(8,128)S(1)}, f32[1,256,256]{2,1,0:T(8,128)}, u32[]{:S(2)}) copy-start(f32[1,256,256]{2,1,0:T(8,128)} %param.10) | copy-start | bytes 786436
